TPU v7x, 32 devices: a whole 2x2x4 slice. The times are simulated.
32 devices in a mesh: pq: 2 (over x), rs: 16 (over z, y, core).
Axes of the slice: x: 2, y: 2, z: 4, core: 2. Of those that a mesh axis runs over, the one named last changes fastest.
Arguments:
- integrals: bfloat16 [128, 1152, 1152], P('pq', 'rs'), may hold values from -6 to 6
- coeff: bfloat16 [1152, 896], P('rs', 'pq'), may hold values from -0.1875 to 0.1875
Outputs:
- half_mo: bfloat16 [128, 896, 896], P('pq', 'rs')
All inputs are finite; a program needn't handle non-finite values.
Results may differ from a plain program's by a relative error of at most 0.0049.
Values may be sent and summed in bfloat16 or wider, within the bound.
A program may use at most 128 MiB of HBM per device.

v0:
```python
import jax
import jax.numpy as jnp
from jax import lax
from jax.sharding import PartitionSpec as P

NBASIS = 1152
NORB = 896


def second_half(received, panel):
    return jnp.einsum("prl,rk->plk", received, panel, preferred_element_type=jnp.float32).astype(
        jnp.bfloat16
    )


def on_device(integrals, coeff):
    pair_rows = integrals.shape[0]
    block_rows = integrals.shape[1]
    flat = integrals.reshape(pair_rows * block_rows, NBASIS)
    strip = lax.all_gather(coeff, "pq", axis=1, tiled=True)
    panel = lax.all_gather(strip, "rs", axis=0, tiled=True)
    first = jnp.dot(flat, panel, preferred_element_type=jnp.float32).astype(jnp.bfloat16)
    first = first.reshape(pair_rows, block_rows, NORB)
    return second_half(lax.all_to_all(first, "rs", split_axis=2, concat_axis=1, tiled=True), panel)


def solution(mesh):
    placed = (P("pq", "rs", None), P("rs", "pq"))
    return jax.shard_map(
        on_device, mesh=mesh, in_specs=placed, out_specs=P("pq", "rs", None), check_vma=False
    )
```

profile of v0, /device:TPU:1, one launch (start us, length us, event | category | flops | bytes accessed | tf_op | source)
XLA Modules:
  0.0 468.6 jit_solution(1243256376461925950)
XLA Ops:
  6.5 0.0 all-gather.3.cloned.1.call-start
  6.5 4.7 %all-gather = bf16[2,448,72]{1,2,0:T(8,128)(2,1)S(1)} all-gather(bf16[1,448,72]{1,2,0:T(8,128)(2,1)} %bitcast.25), channel_id=1, replica_groups=mesh['pq'=2,'rs'=16] {'pq'}, dimensions={0}, use_global_device_ids=true | all-gather | bytes 193536 | tf_op jit(solution)/shard_map/all_gather | solution.py:20
  11.2 0.1 copy.7
  11.3 0.8 reshape.9
  12.1 0.0 all-gather.3.cloned.1.call-update
  12.2 44.5 %all-gather.3.cloned.1.call-done = bf16[1152,896]{1,0:T(8,128)(2,1)} async-done(((bf16[72,896]{1,0:T(8,128)(2,1)}), bf16[1152,896]{1,0:T(8,128)(2,1)}) %all-gather.3.cloned.1.call-update) | async-done | bytes 2064400 | tf_op jit(solution)/shard_map/all_gather | solution.py:21
  56.7 17.5 %convolution_convert_fusion = bf16[4608,896]{1,0:T(8,128)(2,1)} fusion(bf16[4608,1152]{1,0:T(8,128)(2,1)} %bitcast.26, bf16[1152,896]{1,0:T(8,128)(2,1)} %all-gather.3.cloned.1.call-done), kind=kOutput, calls=%fused_computation | convolution fusion | flops 9516810240 | bytes 20938752 | tf_op jit(solution)/shard_map/dot_general | solution.py:22
  74.2 18.5 %copy.8 = bf16[64,72,896]{1,0,2:T(8,128)(2,1)} copy(bf16[64,72,896]{2,1,0:T(8,128)(2,1)} %bitcast.23) | data formatting | bytes 16515072 | tf_op jit(solution)/shard_map/reshape | solution.py:23
  92.7 321.5 %all_to_all.18 = bf16[64,72,896]{1,0,2:T(8,128)(2,1)S(1)} all-to-all(bf16[64,72,896]{1,0,2:T(8,128)(2,1)} %copy.8), channel_id=1, replica_groups=mesh['pq'=2,'rs'=16] {'rs'}, dimensions={2} | all-to-all | bytes 16515072 | tf_op jit(solution)/shard_map/all_to_all | solution.py:24
  414.1 10.6 %copy.10 = bf16[64,16,72,56]{2,1,3,0:T(8,128)(2,1)} copy(bf16[64,16,72,56]{2,0,3,1:T(8,128)(2,1)S(1)} %bitcast.22) | data formatting | bytes 16515072 | tf_op jit(solution)/shard_map/all_to_all | solution.py:24
  424.7 0.0 copy-start
  424.7 23.2 %all_to_all.16 = bf16[64,1152,56]{1,2,0:T(8,128)(2,1)} reshape(bf16[64,16,72,56]{2,1,3,0:T(8,128)(2,1)} %copy.10) | data formatting | bytes 16515072 | tf_op jit(solution)/shard_map/all_to_all | solution.py:24
  447.9 0.0 copy-done
  447.9 13.8 %convolution_convert_fusion.1 = bf16[64,56,896]{2,1,0:T(8,128)(2,1)} fusion(bf16[64,1152,56]{1,2,0:T(8,128)(2,1)} %all_to_all.16, bf16[1152,896]{1,0:T(8,128)(2,1)S(1)} %copy-done), kind=kOutput, calls=%fused_computation.1 | convolution fusion | flops 7401963520 | bytes 16744448 | tf_op jit(solution)/shard_map/prl,rk->plk/dot_general | solution.py:11
Async XLA Ops:
  6.5 50.2 %all-gather.3.cloned.1.call-start = ((), (), s32[]{:S(2)}) async-start(), calls=%async_computation.1 | async-start | bytes 2193408 | tf_op jit(solution)/shard_map/all_gather | solution.py:21
  424.7 23.2 %copy-start = (bf16[1152,896]{1,0:T(8,128)(2,1)S(1)}, bf16[1152,896]{1,0:T(8,128)(2,1)}, u32[]{:S(2)}) copy-start(bf16[1152,896]{1,0:T(8,128)(2,1)} %all-gather.3.cloned.1.call-done) | copy-start | bytes 6193156
Sparse Core Ops, SparseCore 0:
  12.3 44.3 all-gather.2
where the time goes:
time: 470 us; the launch traced here: 469 us
  blocking collectives  326 us (69%)
  local copies, waits for them, and re-layouts  53.2 us (11%)
  waiting for transfers between devices  44.6 us (9%)
  matrix products  31.3 us (7%)
  between operations  13.4 us (3%)
    all_to_all x1, blocking collectives, on_device(): lax.all_to_all(first, 'rs', split_axis=2, concat_axis=1, tiled=True)  321 us
    all_gather x1, waiting for transfers between devices, on_device(): panel = lax.all_gather(strip, 'rs', axis=0, tiled=True)  44.5 us
    all_to_all x2, local copies, waits for them, and re-layouts, on_device(): lax.all_to_all(first, 'rs', split_axis=2, concat_axis=1, tiled=True)  33.8 us
    reshape x1, local copies, waits for them, and re-layouts, on_device(): first = first.reshape(pair_rows, block_rows, NORB)  18.5 us
    dot_general x1, matrix products, on_device(): jnp.dot(flat, panel, preferred_element_type=jnp.float32)  17.5 us
    dot_general x1, matrix products, second_half(): jnp.einsum('prl,rk->plk', received, panel, preferred_element_type=jnp.flo...  13.8 us
  transfers between devices with their start and end apart: 1, of which 1 were waited for; matrix products, arithmetic and copies ran while one was open for 0% of the time, Pallas kernels for 0%

commit v1 on v0

--- a/solution.py
+++ b/solution.py
@@ -18,7 +18,12 @@
     block_rows = integrals.shape[1]
     flat = integrals.reshape(pair_rows * block_rows, NBASIS)
     strip = lax.all_gather(coeff, "pq", axis=1, tiled=True)
-    panel = lax.all_gather(strip, "rs", axis=0, tiled=True)
+    ring = [strip]
+    for hop in range(15):
+        ring.append(lax.ppermute(ring[-1], "rs", [(dev, (dev + 1) % 16) for dev in range(16)]))
+    panel = jnp.roll(
+        jnp.concatenate(ring[::-1], axis=0), (lax.axis_index("rs") + 1) * ring[0].shape[0], axis=0
+    )
     first = jnp.dot(flat, panel, preferred_element_type=jnp.float32).astype(jnp.bfloat16)
     first = first.reshape(pair_rows, block_rows, NORB)
     return second_half(lax.all_to_all(first, "rs", split_axis=2, concat_axis=1, tiled=True), panel)

time: 470 us -> 532 us (1.13)
  waiting for transfers between devices: 44.6 us -> 93.3 us
  local copies, waits for them, and re-layouts: 53.2 us -> 66.4 us
  between operations: 13.4 us -> 0.22 us
  starting transfers between devices: 0.01 us -> 8.11 us
  blocking collectives: 326 us -> 332 us
    ppermute x0 -> x15, waiting for transfers between devices: none -> 93.3 us  [on_device(): lax.ppermute(ring[-1], 'rs', [(dev, (dev + 1) % 16) for dev in range(16)])]
    all_gather x1 -> x0, waiting for transfers between devices: 44.5 us -> none  [on_device(): panel = lax.all_gather(strip, 'rs', axis=0, tiled=True)]
    convert_element_type x0 -> x1, local copies, waits for them, and re-layouts: none -> 11.5 us  [on_device(): jnp.dot(flat, panel, preferred_element_type=jnp.float32)]
    ppermute x0 -> x15, starting transfers between devices: none -> 8.11 us  [on_device(): lax.ppermute(ring[-1], 'rs', [(dev, (dev + 1) % 16) for dev in range(16)])]
    all_to_all x1, blocking collectives: 321 us -> 327 us  [on_device(): lax.all_to_all(first, 'rs', split_axis=2, concat_axis=1, tiled=True)]
  transfers between devices with their start and end apart: 1 -> 15, of which waited for: 1 -> 15; matrix products, arithmetic and copies ran while one was open for 0% -> 0% of each run, Pallas kernels for 0% -> 0%
where the time goes in v1:
time: 532 us; the launch traced here: 530 us
  blocking collectives  332 us (62%)
  waiting for transfers between devices  93.3 us (18%)
  local copies, waits for them, and re-layouts  66.4 us (12%)
  matrix products  30.2 us (6%)
  starting transfers between devices  8.11 us (2%)
    all_to_all x1, blocking collectives, on_device(): lax.all_to_all(first, 'rs', split_axis=2, concat_axis=1, tiled=True)  327 us
    ppermute x15, waiting for transfers between devices, on_device(): lax.ppermute(ring[-1], 'rs', [(dev, (dev + 1) % 16) for dev in range(16)])  93.3 us
    all_to_all x2, local copies, waits for them, and re-layouts, on_device(): lax.all_to_all(first, 'rs', split_axis=2, concat_axis=1, tiled=True)  33.6 us
    reshape x1, local copies, waits for them, and re-layouts, on_device(): first = first.reshape(pair_rows, block_rows, NORB)  18.5 us
    dot_general x1, matrix products, on_device(): jnp.dot(flat, panel, preferred_element_type=jnp.float32)  15.6 us
    dot_general x1, matrix products, second_half(): jnp.einsum('prl,rk->plk', received, panel, preferred_element_type=jnp.flo...  14.5 us
    convert_element_type x1, local copies, waits for them, and re-layouts, on_device(): jnp.dot(flat, panel, preferred_element_type=jnp.float32)  11.5 us
  transfers between devices with their start and end apart: 15, of which 15 were waited for; matrix products, arithmetic and copies ran while one was open for 0% of the time, Pallas kernels for 0%

profile of v1, /device:TPU:1, one launch (start us, length us, event | category | flops | bytes accessed | tf_op | source)
XLA Modules:
  0.0 530.3 jit_solution(15003028117703383906)
XLA Ops:
  0.0 4.7 all-gather
  5.0 3.2 collective-permute-start
  10.1 2.4 collective-permute-start.1
  14.5 2.4 collective-permute-start.2
  16.9 4.6 collective-permute-done.2
  21.5 7.1 %collective-permute-done.3 = bf16[72,896]{1,0:T(8,128)(2,1)S(1)} collective-permute-done((bf16[72,896]{1,0:T(8,128)(2,1)S(1)}, bf16[72,896]{1,0:T(8,128)(2,1)S(1)}, u32[]{:S(2)}, u32[]{:S(2)}) %collective-permute-start.3) | collective-permute-done | bytes 129056 | tf_op jit(solution)/shard_map/ppermute | solution.py:23
  28.6 7.1 %collective-permute-done.4 = bf16[72,896]{1,0:T(8,128)(2,1)S(1)} collective-permute-done((bf16[72,896]{1,0:T(8,128)(2,1)S(1)}, bf16[72,896]{1,0:T(8,128)(2,1)S(1)}, u32[]{:S(2)}, u32[]{:S(2)}) %collective-permute-start.4) | collective-permute-done | bytes 129056 | tf_op jit(solution)/shard_map/ppermute | solution.py:23
  35.7 7.1 %collective-permute-done.5 = bf16[72,896]{1,0:T(8,128)(2,1)S(1)} collective-permute-done((bf16[72,896]{1,0:T(8,128)(2,1)S(1)}, bf16[72,896]{1,0:T(8,128)(2,1)S(1)}, u32[]{:S(2)}, u32[]{:S(2)}) %collective-permute-start.5) | collective-permute-done | bytes 129056 | tf_op jit(solution)/shard_map/ppermute | solution.py:23
  42.7 7.1 %collective-permute-done.6 = bf16[72,896]{1,0:T(8,128)(2,1)S(1)} collective-permute-done((bf16[72,896]{1,0:T(8,128)(2,1)S(1)}, bf16[72,896]{1,0:T(8,128)(2,1)S(1)}, u32[]{:S(2)}, u32[]{:S(2)}) %collective-permute-start.6) | collective-permute-done | bytes 129056 | tf_op jit(solution)/shard_map/ppermute | solution.py:23
  49.8 7.1 %collective-permute-done.7 = bf16[72,896]{1,0:T(8,128)(2,1)S(1)} collective-permute-done((bf16[72,896]{1,0:T(8,128)(2,1)S(1)}, bf16[72,896]{1,0:T(8,128)(2,1)S(1)}, u32[]{:S(2)}, u32[]{:S(2)}) %collective-permute-start.7) | collective-permute-done | bytes 129056 | tf_op jit(solution)/shard_map/ppermute | solution.py:23
  56.9 7.1 %collective-permute-done.8 = bf16[72,896]{1,0:T(8,128)(2,1)S(1)} collective-permute-done((bf16[72,896]{1,0:T(8,128)(2,1)S(1)}, bf16[72,896]{1,0:T(8,128)(2,1)S(1)}, u32[]{:S(2)}, u32[]{:S(2)}) %collective-permute-start.8) | collective-permute-done | bytes 129056 | tf_op jit(solution)/shard_map/ppermute | solution.py:23
  63.9 7.1 %collective-permute-done.9 = bf16[72,896]{1,0:T(8,128)(2,1)S(1)} collective-permute-done((bf16[72,896]{1,0:T(8,128)(2,1)S(1)}, bf16[72,896]{1,0:T(8,128)(2,1)S(1)}, u32[]{:S(2)}, u32[]{:S(2)}) %collective-permute-start.9) | collective-permute-done | bytes 129056 | tf_op jit(solution)/shard_map/ppermute | solution.py:23
  71.0 7.1 %collective-permute-done.10 = bf16[72,896]{1,0:T(8,128)(2,1)S(1)} collective-permute-done((bf16[72,896]{1,0:T(8,128)(2,1)S(1)}, bf16[72,896]{1,0:T(8,128)(2,1)S(1)}, u32[]{:S(2)}, u32[]{:S(2)}) %collective-permute-start.10) | collective-permute-done | bytes 129056 | tf_op jit(solution)/shard_map/ppermute | solution.py:23
  78.1 7.1 %collective-permute-done.11 = bf16[72,896]{1,0:T(8,128)(2,1)S(1)} collective-permute-done((bf16[72,896]{1,0:T(8,128)(2,1)S(1)}, bf16[72,896]{1,0:T(8,128)(2,1)S(1)}, u32[]{:S(2)}, u32[]{:S(2)}) %collective-permute-start.11) | collective-permute-done | bytes 129056 | tf_op jit(solution)/shard_map/ppermute | solution.py:23
  85.1 7.1 %collective-permute-done.12 = bf16[72,896]{1,0:T(8,128)(2,1)S(1)} collective-permute-done((bf16[72,896]{1,0:T(8,128)(2,1)S(1)}, bf16[72,896]{1,0:T(8,128)(2,1)S(1)}, u32[]{:S(2)}, u32[]{:S(2)}) %collective-permute-start.12) | collective-permute-done | bytes 129056 | tf_op jit(solution)/shard_map/ppermute | solution.py:23
  92.2 7.1 %collective-permute-done.13 = bf16[72,896]{1,0:T(8,128)(2,1)S(1)} collective-permute-done((bf16[72,896]{1,0:T(8,128)(2,1)S(1)}, bf16[72,896]{1,0:T(8,128)(2,1)S(1)}, u32[]{:S(2)}, u32[]{:S(2)}) %collective-permute-start.13) | collective-permute-done | bytes 129056 | tf_op jit(solution)/shard_map/ppermute | solution.py:23
  99.3 7.1 %collective-permute-done.14 = bf16[72,896]{1,0:T(8,128)(2,1)S(1)} collective-permute-done((bf16[72,896]{1,0:T(8,128)(2,1)S(1)}, bf16[72,896]{1,0:T(8,128)(2,1)S(1)}, u32[]{:S(2)}, u32[]{:S(2)}) %collective-permute-start.14) | collective-permute-done | bytes 129056 | tf_op jit(solution)/shard_map/ppermute | solution.py:23
  109.1 15.6 %fusion = bf16[4608,896]{0,1:T(8,128)(2,1)} fusion(bf16[4608,1152]{1,0:T(8,128)(2,1)} %bitcast.29, bf16[2304,896]{1,0:T(8,128)(2,1)S(1)} %constant_dynamic-update-slice_fusion, s32[]{:T(128)S(6)} %select_n.14), kind=kOutput, calls=%fused_computation.1 | convolution fusion | flops 9516810240 | bytes 20938756 | tf_op jit(solution)/shard_map/dot_general | solution.py:27
  124.8 11.5 %copy.12 = bf16[4608,896]{1,0:T(8,128)(2,1)} copy(bf16[4608,896]{0,1:T(8,128)(2,1)} %fusion) | data formatting | bytes 16515072 | tf_op jit(solution)/shard_map/convert_element_type | solution.py:27
  136.3 18.5 %copy.13 = bf16[64,72,896]{1,0,2:T(8,128)(2,1)} copy(bf16[64,72,896]{2,1,0:T(8,128)(2,1)} %bitcast.26) | data formatting | bytes 16515072 | tf_op jit(solution)/shard_map/reshape | solution.py:28
  154.8 327.4 %all_to_all.18 = bf16[64,72,896]{1,0,2:T(8,128)(2,1)S(1)} all-to-all(bf16[64,72,896]{1,0,2:T(8,128)(2,1)} %copy.13), channel_id=1, replica_groups=mesh['pq'=2,'rs'=16] {'rs'}, dimensions={2} | all-to-all | bytes 16515072 | tf_op jit(solution)/shard_map/all_to_all | solution.py:29
  482.2 10.5 %copy.15 = bf16[64,16,72,56]{2,1,3,0:T(8,128)(2,1)} copy(bf16[64,16,72,56]{2,0,3,1:T(8,128)(2,1)S(1)} %bitcast.25) | data formatting | bytes 16515072 | tf_op jit(solution)/shard_map/all_to_all | solution.py:29
  492.7 23.1 %all_to_all.16 = bf16[64,1152,56]{1,2,0:T(8,128)(2,1)} reshape(bf16[64,16,72,56]{2,1,3,0:T(8,128)(2,1)} %copy.15) | data formatting | bytes 16515072 | tf_op jit(solution)/shard_map/all_to_all | solution.py:29
  515.7 14.5 %convolution_convert_fusion.1 = bf16[64,56,896]{2,1,0:T(8,128)(2,1)} fusion(bf16[64,1152,56]{1,2,0:T(8,128)(2,1)} %all_to_all.16, bf16[2304,896]{1,0:T(8,128)(2,1)} %copy-done, s32[]{:T(128)S(6)} %select_n.14), kind=kOutput, calls=%fused_computation.2 | convolution fusion | flops 7401963520 | bytes 16744452 | tf_op jit(solution)/shard_map/prl,rk->plk/dot_general | solution.py:11
  (50 shorter events, 6.7 us)
Async XLA Ops:
  5.0 5.1 collective-permute-start
  10.1 4.4 collective-permute-start.1
  14.5 7.1 %collective-permute-start.2 = (bf16[72,896]{1,0:T(8,128)(2,1)S(1)}, bf16[72,896]{1,0:T(8,128)(2,1)S(1)}, u32[]{:S(2)}, u32[]{:S(2)}) collective-permute-start(bf16[72,896]{1,0:T(8,128)(2,1)S(1)} %collective-permute-done.1), channel_id=1, source_target_pairs={{0,1},{1,2},{2,3},{3,4},{4,5},{5,6},{6,7},{7,8},{8,9},{9,10},{10,1... | collective-permute-start | bytes 387080 | tf_op jit(solution)/shard_map/ppermute | solution.py:23
  21.5 7.1 %collective-permute-start.3 = (bf16[72,896]{1,0:T(8,128)(2,1)S(1)}, bf16[72,896]{1,0:T(8,128)(2,1)S(1)}, u32[]{:S(2)}, u32[]{:S(2)}) collective-permute-start(bf16[72,896]{1,0:T(8,128)(2,1)S(1)} %collective-permute-done.2), channel_id=1, source_target_pairs={{0,1},{1,2},{2,3},{3,4},{4,5},{5,6},{6,7},{7,8},{8,9},{9,10},{10,1... | collective-permute-start | bytes 387080 | tf_op jit(solution)/shard_map/ppermute | solution.py:23
  28.6 7.1 %collective-permute-start.4 = (bf16[72,896]{1,0:T(8,128)(2,1)S(1)}, bf16[72,896]{1,0:T(8,128)(2,1)S(1)}, u32[]{:S(2)}, u32[]{:S(2)}) collective-permute-start(bf16[72,896]{1,0:T(8,128)(2,1)S(1)} %collective-permute-done.3), channel_id=1, source_target_pairs={{0,1},{1,2},{2,3},{3,4},{4,5},{5,6},{6,7},{7,8},{8,9},{9,10},{10,1... | collective-permute-start | bytes 387080 | tf_op jit(solution)/shard_map/ppermute | solution.py:23
  35.7 7.1 %collective-permute-start.5 = (bf16[72,896]{1,0:T(8,128)(2,1)S(1)}, bf16[72,896]{1,0:T(8,128)(2,1)S(1)}, u32[]{:S(2)}, u32[]{:S(2)}) collective-permute-start(bf16[72,896]{1,0:T(8,128)(2,1)S(1)} %collective-permute-done.4), channel_id=1, source_target_pairs={{0,1},{1,2},{2,3},{3,4},{4,5},{5,6},{6,7},{7,8},{8,9},{9,10},{10,1... | collective-permute-start | bytes 387080 | tf_op jit(solution)/shard_map/ppermute | solution.py:23
  42.7 7.1 %collective-permute-start.6 = (bf16[72,896]{1,0:T(8,128)(2,1)S(1)}, bf16[72,896]{1,0:T(8,128)(2,1)S(1)}, u32[]{:S(2)}, u32[]{:S(2)}) collective-permute-start(bf16[72,896]{1,0:T(8,128)(2,1)S(1)} %collective-permute-done.5), channel_id=1, source_target_pairs={{0,1},{1,2},{2,3},{3,4},{4,5},{5,6},{6,7},{7,8},{8,9},{9,10},{10,1... | collective-permute-start | bytes 387080 | tf_op jit(solution)/shard_map/ppermute | solution.py:23
  49.8 7.1 %collective-permute-start.7 = (bf16[72,896]{1,0:T(8,128)(2,1)S(1)}, bf16[72,896]{1,0:T(8,128)(2,1)S(1)}, u32[]{:S(2)}, u32[]{:S(2)}) collective-permute-start(bf16[72,896]{1,0:T(8,128)(2,1)S(1)} %collective-permute-done.6), channel_id=1, source_target_pairs={{0,1},{1,2},{2,3},{3,4},{4,5},{5,6},{6,7},{7,8},{8,9},{9,10},{10,1... | collective-permute-start | bytes 387080 | tf_op jit(solution)/shard_map/ppermute | solution.py:23
  56.9 7.1 %collective-permute-start.8 = (bf16[72,896]{1,0:T(8,128)(2,1)S(1)}, bf16[72,896]{1,0:T(8,128)(2,1)S(1)}, u32[]{:S(2)}, u32[]{:S(2)}) collective-permute-start(bf16[72,896]{1,0:T(8,128)(2,1)S(1)} %collective-permute-done.7), channel_id=1, source_target_pairs={{0,1},{1,2},{2,3},{3,4},{4,5},{5,6},{6,7},{7,8},{8,9},{9,10},{10,1... | collective-permute-start | bytes 387080 | tf_op jit(solution)/shard_map/ppermute | solution.py:23
  63.9 7.1 %collective-permute-start.9 = (bf16[72,896]{1,0:T(8,128)(2,1)S(1)}, bf16[72,896]{1,0:T(8,128)(2,1)S(1)}, u32[]{:S(2)}, u32[]{:S(2)}) collective-permute-start(bf16[72,896]{1,0:T(8,128)(2,1)S(1)} %collective-permute-done.8), channel_id=1, source_target_pairs={{0,1},{1,2},{2,3},{3,4},{4,5},{5,6},{6,7},{7,8},{8,9},{9,10},{10,1... | collective-permute-start | bytes 387080 | tf_op jit(solution)/shard_map/ppermute | solution.py:23
  71.0 7.1 %collective-permute-start.10 = (bf16[72,896]{1,0:T(8,128)(2,1)S(1)}, bf16[72,896]{1,0:T(8,128)(2,1)S(1)}, u32[]{:S(2)}, u32[]{:S(2)}) collective-permute-start(bf16[72,896]{1,0:T(8,128)(2,1)S(1)} %collective-permute-done.9), channel_id=1, source_target_pairs={{0,1},{1,2},{2,3},{3,4},{4,5},{5,6},{6,7},{7,8},{8,9},{9,10},{10,1... | collective-permute-start | bytes 387080 | tf_op jit(solution)/shard_map/ppermute | solution.py:23
  78.1 7.1 %collective-permute-start.11 = (bf16[72,896]{1,0:T(8,128)(2,1)S(1)}, bf16[72,896]{1,0:T(8,128)(2,1)S(1)}, u32[]{:S(2)}, u32[]{:S(2)}) collective-permute-start(bf16[72,896]{1,0:T(8,128)(2,1)S(1)} %collective-permute-done.10), channel_id=1, source_target_pairs={{0,1},{1,2},{2,3},{3,4},{4,5},{5,6},{6,7},{7,8},{8,9},{9,10},{10,1... | collective-permute-start | bytes 387080 | tf_op jit(solution)/shard_map/ppermute | solution.py:23
  85.1 7.1 %collective-permute-start.12 = (bf16[72,896]{1,0:T(8,128)(2,1)S(1)}, bf16[72,896]{1,0:T(8,128)(2,1)S(1)}, u32[]{:S(2)}, u32[]{:S(2)}) collective-permute-start(bf16[72,896]{1,0:T(8,128)(2,1)S(1)} %collective-permute-done.11), channel_id=1, source_target_pairs={{0,1},{1,2},{2,3},{3,4},{4,5},{5,6},{6,7},{7,8},{8,9},{9,10},{10,1... | collective-permute-start | bytes 387080 | tf_op jit(solution)/shard_map/ppermute | solution.py:23
  92.2 7.1 %collective-permute-start.13 = (bf16[72,896]{1,0:T(8,128)(2,1)S(1)}, bf16[72,896]{1,0:T(8,128)(2,1)S(1)}, u32[]{:S(2)}, u32[]{:S(2)}) collective-permute-start(bf16[72,896]{1,0:T(8,128)(2,1)S(1)} %collective-permute-done.12), channel_id=1, source_target_pairs={{0,1},{1,2},{2,3},{3,4},{4,5},{5,6},{6,7},{7,8},{8,9},{9,10},{10,1... | collective-permute-start | bytes 387080 | tf_op jit(solution)/shard_map/ppermute | solution.py:23
  99.3 7.1 %collective-permute-start.14 = (bf16[72,896]{1,0:T(8,128)(2,1)S(1)}, bf16[72,896]{1,0:T(8,128)(2,1)S(1)}, u32[]{:S(2)}, u32[]{:S(2)}) collective-permute-start(bf16[72,896]{1,0:T(8,128)(2,1)S(1)} %collective-permute-done.13), channel_id=1, source_target_pairs={{0,1},{1,2},{2,3},{3,4},{4,5},{5,6},{6,7},{7,8},{8,9},{9,10},{10,1... | collective-permute-start | bytes 387080 | tf_op jit(solution)/shard_map/ppermute | solution.py:23
  107.1 2.0 copy-start
